TPU v7x, 512 devices: a whole 4x8x8 slice. The times are simulated.
512 devices in a mesh: tp: 8 (over y), row: 8 (over z_hi, x), col: 8 (over z_lo, core).
Axes of the slice: x: 4, y: 8, z: 8 (z_hi: 2, z_lo: 4; z = z_hi * 4 + z_lo), core: 2. Of those that a mesh axis runs over, the one named last changes fastest.
Arguments:
- hidden: bfloat16 [128, 14336], P('col', 'row'), may hold values from -6 to 6
- out_grad: bfloat16 [128, 4096], P(None, ('tp', 'row')), may hold values from -6 to 6
- basis_in: bfloat16 [14336, 4096], P(('row', 'col'), 'tp'), may hold values from -0.046875 to 0.046875
- basis_out: bfloat16 [4096, 1024], P(('tp', 'row'), 'col'), may hold values from -0.09375 to 0.09375
- eigen: float32 [4096, 1024], P(('tp', 'row'), 'col'), may hold values from 0.02 to 2
Outputs:
- precond: float32 [4096, 14336], P(('tp', 'col'), 'row')
All inputs are finite; a program needn't handle non-finite values.
Results may differ from a plain program's by a relative error of at most 0.024.
Values may be sent and summed in bfloat16 or wider, within the bound.
A program may use at most 64 MiB of HBM per device.

v0:
```python
import jax
import jax.numpy as jnp
from jax import lax
from jax.sharding import PartitionSpec as P

damping = 0.01


def sent_to_all(array, axis):
    devices = lax.axis_size(axis)
    return lax.all_to_all(
        jnp.broadcast_to(array[None], (devices, *array.shape)), axis, 0, 0, tiled=True
    )


def laid_out(tiles, dim):
    dims = list(tiles.shape[1:])
    dims[dim] *= tiles.shape[0]
    return jnp.moveaxis(tiles, 0, dim).reshape(dims)


def gathered_copies(array, axis, dim):
    tiles = sent_to_all(array, axis)
    return laid_out(tiles, dim)


def in_blocks(array, dim, devices):
    before, after = (array.shape[:dim], array.shape[dim + 1 :])
    return jnp.moveaxis(array.reshape(*before, devices, -1, *after), dim, 0)


def sent_and_summed(array, axis, dim):
    tiles = in_blocks(array, dim, lax.axis_size(axis))
    arrived = lax.all_to_all(tiles, axis, split_axis=0, concat_axis=0, tiled=True)
    return arrived.astype(jnp.float32).sum(axis=0)


def contract_rows(left, right):
    return lax.dot_general(
        left, right, (((0,), (0,)), ((), ())), preferred_element_type=jnp.float32
    )


def contract_cols(left, right):
    return lax.dot_general(
        left, right, (((1,), (1,)), ((), ())), preferred_element_type=jnp.float32
    )


def shards(hidden, out_grad, basis_in, basis_out, eigen):
    tp_count = lax.axis_size("tp")
    col_count = lax.axis_size("col")
    basis_block = gathered_copies(basis_in, "col", 0)
    partial_in = jnp.dot(hidden, basis_block, preferred_element_type=jnp.float32)
    rotated_in = sent_and_summed(partial_in.astype(jnp.bfloat16), "row", 1).astype(jnp.bfloat16)
    rotated_in = gathered_copies(rotated_in, "col", 0)
    queries = rotated_in.shape[0]
    out_rows = gathered_copies(basis_out, ("tp", "row"), 0)
    grad_full = lax.all_gather(out_grad, ("tp", "row"), axis=1, tiled=True)
    rotated_out = jnp.dot(grad_full, out_rows, preferred_element_type=jnp.float32).astype(
        jnp.bfloat16
    )
    coeff = contract_rows(rotated_in, rotated_out)
    scaled = (coeff / (queries * (eigen + damping))).astype(jnp.bfloat16)
    mixed_part = contract_cols(scaled, out_rows)
    depth = mixed_part.shape[0]
    width = mixed_part.shape[1]
    mixed_part = mixed_part.reshape(depth, tp_count, col_count, width // (tp_count * col_count))
    mixed = sent_and_summed(mixed_part.astype(jnp.bfloat16), "col", 2)
    mixed = mixed.reshape(depth, width // col_count).astype(jnp.bfloat16)
    mixed = gathered_copies(mixed, "row", 0)
    return sent_and_summed(
        lax.dot_general(
            mixed, basis_block, (((0,), (1,)), ((), ())), preferred_element_type=jnp.float32
        ).astype(jnp.bfloat16),
        "tp",
        0,
    )


def solution(mesh):
    placed = (
        P("col", "row"),
        P(None, ("tp", "row")),
        P(("row", "col"), "tp"),
        P(("tp", "row"), "col"),
        P(("tp", "row"), "col"),
    )
    return jax.shard_map(
        shards, mesh=mesh, in_specs=placed, out_specs=P(("tp", "col"), "row"), check_vma=False
    )
```

profile of v0, /device:TPU:1, one launch (start us, length us, event | category | flops | bytes accessed | tf_op | source)
XLA Modules:
  0.0 332.6 jit_solution(7538081881652696159)
XLA Ops:
  6.5 1.1 broadcast_in_dim.8
  7.6 51.7 %all_to_all.35 = bf16[8,224,512]{2,1,0:T(8,128)(2,1)S(1)} all-to-all(bf16[8,224,512]{2,1,0:T(8,128)(2,1)S(1)} %broadcast_in_dim.8), channel_id=1, replica_groups=mesh['tp'=8,'row'=8,'col'=8] {'col'}, dimensions={0} | all-to-all | bytes 3670016 | tf_op jit(solution)/shard_map/all_to_all | solution.py:11
  59.3 0.3 convolution_convert_fusion.3
  59.6 0.1 reshape.37
  59.8 0.1 reshape.44
  59.9 17.8 %all_to_all.36 = bf16[8,2,512]{2,1,0:T(2,128)(2,1)S(1)} all-to-all(bf16[8,2,512]{2,1,0:T(2,128)(2,1)S(1)} %reshape.44), channel_id=1, replica_groups=mesh['tp'=8,'row'=8,'col'=8] {'row'}, dimensions={0} | all-to-all | bytes 32768 | tf_op jit(solution)/shard_map/all_to_all | solution.py:34
  77.8 0.1 reshape.46
  77.9 9.8 %all_to_all.37 = bf16[8,2,512]{2,1,0:T(2,128)(2,1)S(1)} all-to-all(bf16[8,2,512]{2,1,0:T(2,128)(2,1)S(1)} %reshape.46), channel_id=1, replica_groups=mesh['tp'=8,'row'=8,'col'=8] {'col'}, dimensions={0} | all-to-all | bytes 32768 | tf_op jit(solution)/shard_map/all_to_all | solution.py:11
  87.7 1.3 broadcast_in_dim.10
  88.9 8.5 %all-to-all-start.3 = ((bf16[64,64,128]{2,1,0:T(8,128)(2,1)}), bf16[64,64,128]{2,1,0:T(8,128)(2,1)S(1)}, u32[]{:S(2)}, u32[]{:S(2)}) async-start(bf16[64,64,128]{2,1,0:T(8,128)(2,1)} %broadcast_in_dim.10), calls=%async_computation.3 | async-start | bytes 2097152 | tf_op jit(solution)/shard_map/all_to_all | solution.py:11
  97.5 0.7 all-gather.2.cloned.1.call-update
  98.3 27.8 %all-to-all-done.3 = bf16[64,64,128]{2,1,0:T(8,128)(2,1)S(1)} async-done(((bf16[64,64,128]{2,1,0:T(8,128)(2,1)}), bf16[64,64,128]{2,1,0:T(8,128)(2,1)S(1)}, u32[]{:S(2)}, u32[]{:S(2)}) %all-to-all-start.3) | async-done | bytes 1048608 | tf_op jit(solution)/shard_map/all_to_all | solution.py:11
  126.1 103.7 %all-gather.2.cloned.1.call-done = bf16[128,4096]{0,1:T(8,128)(2,1)} async-done(((bf16[128,64]{0,1:T(8,128)(2,1)}), bf16[128,4096]{0,1:T(8,128)(2,1)}) %all-gather.2.cloned.1.call-update) | async-done | bytes 1048592 | tf_op jit(solution)/shard_map/all_gather | solution.py:59
  229.8 1.8 fusion.4
  231.6 1.1 fusion
  232.9 0.7 reshape.48
  233.6 23.1 %all_to_all.38 = bf16[8,2,16384]{2,1,0:T(2,128)(2,1)} all-to-all(bf16[8,2,16384]{2,1,0:T(2,128)(2,1)S(1)} %reshape.48), channel_id=1, replica_groups=mesh['tp'=8,'row'=8,'col'=8] {'col'}, dimensions={0} | all-to-all | bytes 1048576 | tf_op jit(solution)/shard_map/all_to_all | solution.py:34
  256.7 2.3 reshape.49
  259.0 0.2 bitcast_reduce_fusion
  259.3 0.1 convert_element_type.33
  259.5 18.7 %all_to_all.39 = bf16[8,64,512]{2,1,0:T(8,128)(2,1)S(1)} all-to-all(bf16[8,64,512]{2,1,0:T(8,128)(2,1)S(1)} %broadcast_in_dim.11), channel_id=1, replica_groups=mesh['tp'=8,'row'=8,'col'=8] {'row'}, dimensions={0} | all-to-all | bytes 1048576 | tf_op jit(solution)/shard_map/all_to_all | solution.py:11
  278.2 1.2 convolution_convert_fusion
  279.4 45.3 %all_to_all.40 = bf16[8,64,1792]{2,1,0:T(8,128)(2,1)S(1)} all-to-all(bf16[8,64,1792]{2,1,0:T(8,128)(2,1)S(1)} %bitcast.36), channel_id=1, replica_groups=mesh['tp'=8,'row'=8,'col'=8] {'tp'}, dimensions={0} | all-to-all | bytes 3670016 | tf_op jit(solution)/shard_map/all_to_all | solution.py:34
  324.7 1.0 convert_reduce_fusion
  (15 shorter events, 0.5 us)
Async XLA Ops:
  6.5 52.8 %copy-start = (bf16[16,1792]{1,0:T(8,128)(2,1)S(1)}, bf16[16,1792]{1,0:T(8,128)(2,1)}, u32[]{:S(2)}) copy-start(bf16[16,1792]{1,0:T(8,128)(2,1)} %param.5) | copy-start | bytes 172036
  59.3 28.4 %copy-start.2 = (bf16[64,128]{1,0:T(8,128)(2,1)S(1)}, bf16[64,128]{1,0:T(8,128)(2,1)}, u32[]{:S(2)}) copy-start(bf16[64,128]{1,0:T(8,128)(2,1)} %param.8) | copy-start | bytes 49156
  59.6 170.2 %copy-start.1 = (f32[64,128]{1,0:T(8,128)S(1)}, f32[64,128]{1,0:T(8,128)}, u32[]{:S(2)}) copy-start(f32[64,128]{1,0:T(8,128)} %param.9) | copy-start | bytes 98308
  88.9 37.1 %all-to-all-start.3 = ((bf16[64,64,128]{2,1,0:T(8,128)(2,1)}), bf16[64,64,128]{2,1,0:T(8,128)(2,1)S(1)}, u32[]{:S(2)}, u32[]{:S(2)}) async-start(bf16[64,64,128]{2,1,0:T(8,128)(2,1)} %broadcast_in_dim.10), calls=%async_computation.3 | async-start | bytes 2097152 | tf_op jit(solution)/shard_map/all_to_all | solution.py:11
  97.4 132.4 %all-gather.2.cloned.1.call-start = ((), (), s32[]{:S(2)}) async-start(), calls=%async_computation.7 | async-start | bytes 1064960 | tf_op jit(solution)/shard_map/all_gather | solution.py:59
Sparse Core Ops, SparseCore 0:
  102.6 127.1 all-gather.1
where the time goes:
time: 335 us; the launch traced here: 333 us
  blocking collectives  166 us (50%)
  waiting for transfers between devices  132 us (39%)
  between operations  13.5 us (4%)
  starting transfers between devices  8.52 us (3%)
  local copies, waits for them, and re-layouts  6.28 us (2%)
  matrix products  4.45 us (1%)
    all_gather x1, waiting for transfers between devices, shards(): grad_full = lax.all_gather(out_grad, ('tp', 'row'), axis=1, tiled=True)  104 us
    all_to_all x3, blocking collectives, sent_and_summed(): lax.all_to_all(tiles, axis, split_axis=0, concat_axis=0, tiled=True)  86.2 us
    all_to_all x3, blocking collectives, sent_to_all(): lax.all_to_all(jnp.broadcast_to(array[None], (devices, *array.shape)), ax...  80.1 us
    all_to_all x1, waiting for transfers between devices, sent_to_all(): lax.all_to_all(jnp.broadcast_to(array[None], (devices, *array.shape)), ax...  27.8 us
    all_to_all x1, starting transfers between devices, sent_to_all(): lax.all_to_all(jnp.broadcast_to(array[None], (devices, *array.shape)), ax...  8.48 us
  transfers between devices with their start and end apart: 2, of which 2 were waited for; matrix products, arithmetic and copies ran while one was open for 0% of the time, Pallas kernels for 0%

commit v1 on v0

v1 whole, which is shorter than its diff:
```python
import functools

import jax
import jax.numpy as jnp
from jax import lax
from jax.experimental import pallas as pl
from jax.experimental.pallas import tpu as pltpu
from jax.sharding import PartitionSpec as P

MESH = pl.DeviceIdType.MESH
BF16 = jnp.bfloat16
F32 = jnp.float32
damping = 0.01
NX, NZ_HI, NZ_LO, NC = 4, 2, 4, 2
NZ = NZ_HI * NZ_LO
NY = 8
SPLIT = 2


def far_first(count):
    return sorted(range(1, count), key=lambda hop: -min(hop, count - hop))


def kernel(
    hidden, out_grad, basis_in, basis_out, eigen, out,
    hid_v, grad_v, eig_v, basis, hid_s, hid_r,
    p_s, p_r, p_x, p_g, rin,
    r_s, r_r, r_y, r_z, r_x,
    e_g, b_g, scaled, w_s, w_1, w_2, w_g, b_full, o_f, o_s, o_r, f_s, f_r,
    load_sem, send_sem, recv_sem,
):
    t = lax.axis_index("tp")
    row = lax.axis_index("row")
    col = lax.axis_index("col")
    z_hi, x = lax.div(row, NX), lax.rem(row, NX)
    z_lo, core = lax.div(col, NC), lax.rem(col, NC)
    z = z_hi * NZ_LO + z_lo

    def at_y(pos):
        return {"tp": pos}

    def at_x(pos):
        return {"row": z_hi * NX + pos}

    def at_z(pos):
        return {
            "row": lax.div(pos, NZ_LO) * NX + x,
            "col": lax.rem(pos, NZ_LO) * NC + core,
        }

    def at_zlo(pos):
        return {"col": pos * NC + core}

    at_core = {"col": z_lo * NC + 1 - core}

    slots = [0]
    sent = []

    def fresh(count):
        first = slots[0]
        slots[0] += count
        return first

    def remote(src, dst, sem, device):
        return pltpu.make_async_remote_copy(
            src_ref=src, dst_ref=dst, send_sem=send_sem.at[sem], recv_sem=recv_sem.at[sem],
            device_id=device, device_id_type=MESH,
        )

    def start(src, dst, sem, device):
        copy = remote(src, dst, sem, device)
        copy.start()
        sent.append(copy)

    def exchange(src, dst, me, count, at):
        first = fresh(count)
        for hop in far_first(count):
            peer = lax.rem(me + hop, count)
            start(src(peer), dst(me), first + hop, at(peer))

        def finish():
            for hop in reversed(far_first(count)):
                sender = lax.rem(me + count - hop, count)
                remote(src(sender), dst(sender), first + hop, at(sender)).wait_recv()

        return finish

    def gather(buf, me, count, at):
        return exchange(lambda peer: buf.at[me], lambda sender: buf.at[sender], me, count, at)

    def scatter(src, dst, me, count, at):
        return exchange(lambda peer: src.at[peer], lambda sender: dst.at[sender], me, count, at)

    def total(buf, count):
        acc = buf[0].astype(F32)
        for i in range(1, count):
            acc = acc + buf[i].astype(F32)
        return acc

    def put(buf, pos, value):
        buf[pl.ds(pos, 1)] = value[None]

    loads = [
        pltpu.make_async_copy(hidden, hid_v, load_sem.at[0]),
        pltpu.make_async_copy(out_grad, grad_v, load_sem.at[1]),
        pltpu.make_async_copy(basis_out, b_g.at[x, z], load_sem.at[2]),
        pltpu.make_async_copy(basis_in, basis.at[core], load_sem.at[3]),
        pltpu.make_async_copy(eigen, eig_v, load_sem.at[4]),
    ]
    for load in loads:
        load.start()

    barrier = pltpu.get_barrier_semaphore()
    partners = [at_core]
    partners += [at_x(lax.rem(x + hop, NX)) for hop in range(1, NX)]
    partners += [at_z(lax.rem(z + hop, NZ)) for hop in range(1, NZ)]
    partners += [at_y(lax.rem(t + hop, NY)) for hop in range(1, NY)]
    for partner in partners:
        pl.semaphore_signal(barrier, inc=1, device_id=partner, device_id_type=MESH)

    own_tok = hid_v.shape[0]
    wide = hid_s.shape[2]
    loads[0].wait()
    hid = hid_v[...]
    for i in range(NZ_LO):
        hid_s[i] = hid[:, i * wide:(i + 1) * wide]
    hid_r[pl.ds(z_lo, 1)] = hid_s[pl.ds(z_lo, 1)]

    loads[1].wait()
    loads[2].wait()
    part = jnp.dot(grad_v[...], b_g[x, z], preferred_element_type=F32)
    order = [i * NC + p for p in range(NC) for i in range(NZ_LO)]
    part = jnp.concatenate([part[i * own_tok:(i + 1) * own_tok] for i in order], axis=0)
    piece = r_s.shape[1]
    for i in range(NX):
        r_s[i] = part[i * piece:(i + 1) * piece].astype(BF16)
    r_r[pl.ds(x, 1)] = r_s[pl.ds(x, 1)]
    loads[3].wait()
    loads[4].wait()
    queries = own_tok * NZ_LO * NC
    e_g[x, z] = (1.0 / (queries * (eig_v[...] + damping))).astype(BF16)

    pl.semaphore_wait(barrier, len(partners))

    hid_done = scatter(hid_s, hid_r, z_lo, NZ_LO, at_zlo)
    basis_sem = fresh(1)
    start(basis.at[core], basis.at[core], basis_sem, at_core)
    r_done = scatter(r_s, r_r, x, NX, at_x)
    ez_done = exchange(
        lambda peer: e_g.at[x, z], lambda sender: e_g.at[x, sender], z, NZ, at_z
    )

    r_done()
    put(r_y, t, total(r_r, NX).astype(BF16))
    ry_done = gather(r_y, t, NY, at_y)

    hid_done()
    remote(basis.at[core], basis.at[1 - core], basis_sem, at_core).wait_recv()
    deep = NC * basis.shape[1]
    basis_rows = basis[...].reshape(deep, basis.shape[2])
    p_full = jnp.dot(
        hid_r[...].reshape(NZ_LO * own_tok, wide), basis_rows, preferred_element_type=F32
    )
    tall, broad = p_s.shape[1:]
    across = basis.shape[2] // broad
    for i in range(NZ):
        h, q = i // across, i % across
        p_s[i] = p_full[h * tall:(h + 1) * tall, q * broad:(q + 1) * broad].astype(BF16)
    p_r[pl.ds(z, 1)] = p_s[pl.ds(z, 1)]
    p_done = scatter(p_s, p_r, z, NZ, at_z)

    ry_done()
    put(r_z, z, total(r_y, NY).astype(BF16))
    rz_done = gather(r_z, z, NZ, at_z)

    p_done()
    put(p_x, x, total(p_r, NZ).astype(BF16))
    px_done = gather(p_x, x, NX, at_x)

    ez_done()
    ex_done = gather(e_g, x, NX, at_x)

    px_done()
    put(p_g, z, total(p_x, NX).astype(BF16))
    pg_done = gather(p_g, z, NZ, at_z)

    rz_done()
    put(
        r_x, x,
        jnp.concatenate(
            [
                sum(r_z[h * NZ_LO + i].astype(F32) for h in range(NZ_HI)).astype(BF16)
                for i in range(NZ_LO)
            ],
            axis=1,
        ),
    )
    rx_done = gather(r_x, x, NX, at_x)

    pg_done()
    put(
        rin, core,
        jnp.concatenate(
            [
                jnp.concatenate([p_g[h * across + q] for q in range(across)], axis=1)
                for h in range(NZ // across)
            ],
            axis=0,
        ),
    )
    rin_sem = fresh(1)
    start(rin.at[core], rin.at[core], rin_sem, at_core)
    bz_done = exchange(
        lambda peer: b_g.at[x, z], lambda sender: b_g.at[x, sender], z, NZ, at_z
    )

    rx_done()
    remote(rin.at[core], rin.at[1 - core], rin_sem, at_core).wait_recv()
    depth = basis.shape[2]
    across_out = NZ_LO * b_g.shape[3]
    coeff = lax.dot_general(
        rin[...].reshape(queries, depth), r_x[...].reshape(queries, across_out),
        (((0,), (0,)), ((), ())), preferred_element_type=F32,
    )
    ex_done()
    rows, cols = b_g.shape[2:]
    for i in range(NX):
        for k in range(NZ):
            h, low = k // NZ_LO, k % NZ_LO
            r0, c0 = (h * NX + i) * rows, low * cols
            scaled[r0:r0 + rows, c0:c0 + cols] = (
                coeff[r0:r0 + rows, c0:c0 + cols] * e_g[i, k].astype(F32)
            ).astype(BF16)

    w_full = jnp.dot(basis_rows, scaled[...], preferred_element_type=F32)
    chunk = w_s.shape[1]
    for i in range(NY):
        w_s[i] = w_full[i * chunk:(i + 1) * chunk].astype(BF16)

    heading = 1 - 2 * core
    ahead = at_y(lax.rem(t + heading + NY, NY))
    behind = at_y(lax.rem(t - heading + NY, NY))
    first_hops, second_hops = NY // 2, NY // 2 - 1
    span = w_s.shape[2] // SPLIT

    def off(steps):
        return lax.rem(t + heading * steps + 2 * NY, NY)

    def cut(buf, slot, q):
        return buf.at[slot, :, pl.ds(q * span, span)]

    def add_in(slot, buf, step, q):
        here = (pl.ds(slot, 1), slice(None), pl.ds(q * span, span))
        there = (pl.ds(step, 1), slice(None), pl.ds(q * span, span))
        w_s[here] = (w_s[here].astype(F32) + buf[there].astype(F32)).astype(BF16)

    sem_1 = fresh(first_hops * SPLIT)
    sem_2 = fresh(second_hops * SPLIT)
    for step in range(first_hops):
        for q in range(SPLIT):
            dest = off(first_hops - step)
            sem = sem_1 + step * SPLIT + q
            if step > 0:
                remote(cut(w_s, dest, q), cut(w_1, step - 1, q), sem - SPLIT, behind).wait_recv()
                add_in(dest, w_1, step - 1, q)
            start(cut(w_s, dest, q), cut(w_1, step, q), sem, ahead)
            if step < second_hops:
                dest = off(step - second_hops)
                sem = sem_2 + step * SPLIT + q
                if step > 0:
                    remote(cut(w_s, dest, q), cut(w_2, step - 1, q), sem - SPLIT, ahead).wait_recv()
                    add_in(dest, w_2, step - 1, q)
                start(cut(w_s, dest, q), cut(w_2, step, q), sem, behind)

    bz_done()
    bx_done = gather(b_g, x, NX, at_x)

    gsem_1 = fresh(first_hops * SPLIT)
    gsem_2 = fresh(second_hops * SPLIT)
    for q in range(SPLIT):
        remote(
            cut(w_s, t, q), cut(w_2, second_hops - 1, q),
            sem_2 + (second_hops - 1) * SPLIT + q, ahead,
        ).wait_recv()
        add_in(t, w_2, second_hops - 1, q)
        remote(
            cut(w_s, t, q), cut(w_1, first_hops - 1, q),
            sem_1 + (first_hops - 1) * SPLIT + q, behind,
        ).wait_recv()
        here = (pl.ds(t, 1), slice(None), pl.ds(q * span, span))
        w_g[here] = (
            w_s[here].astype(F32) + w_1[first_hops - 1, :, q * span:(q + 1) * span].astype(F32)[None]
        ).astype(BF16)
        start(cut(w_g, t, q), cut(w_g, t, q), gsem_1 + q, ahead)
        start(cut(w_g, t, q), cut(w_g, t, q), gsem_2 + q, behind)
    for step in range(1, first_hops + 1):
        for q in range(SPLIT):
            slot = off(-step)
            sem = gsem_1 + step * SPLIT + q
            remote(cut(w_g, slot, q), cut(w_g, slot, q), sem - SPLIT, behind).wait_recv()
            if step < first_hops:
                start(cut(w_g, slot, q), cut(w_g, slot, q), sem, ahead)
            if step <= second_hops:
                slot = off(step)
                sem = gsem_2 + step * SPLIT + q
                remote(cut(w_g, slot, q), cut(w_g, slot, q), sem - SPLIT, ahead).wait_recv()
                if step < second_hops:
                    start(cut(w_g, slot, q), cut(w_g, slot, q), sem, behind)

    bx_done()
    for i in range(NX):
        for k in range(NZ):
            h, low = k // NZ_LO, k % NZ_LO
            r0, c0 = (h * NX + i) * rows, low * cols
            b_full[r0:r0 + rows, c0:c0 + cols] = b_g[i, k]
    w_all = jnp.concatenate([w_g[i] for i in range(NY)], axis=0)
    result = lax.dot_general(
        b_full[...], w_all, (((1,), (1,)), ((), ())), preferred_element_type=F32
    )
    for i in range(NZ_LO * NC):
        o_f[i] = result[i * rows:(i + 1) * rows]
    for i in range(NZ_LO):
        o_s[pl.ds(i, 1)] = o_f[pl.ds(i * NC + 1 - core, 1)].astype(BF16)
    o_sem = fresh(1)
    start(o_s, o_r, o_sem, at_core)
    remote(o_s, o_r, o_sem, at_core).wait_recv()
    for i in range(NZ_LO):
        f_s[pl.ds(i, 1)] = (
            o_f[pl.ds(i * NC + core, 1)] + o_r[i].astype(F32)[None]
        ).astype(BF16)
    f_r[pl.ds(z_lo, 1)] = f_s[pl.ds(z_lo, 1)]
    f_done = scatter(f_s, f_r, z_lo, NZ_LO, at_zlo)
    f_done()
    for i in range(NZ_LO):
        out[:, i * wide:(i + 1) * wide] = f_r[i].astype(F32)
    for copy in sent:
        copy.wait_send()


def shards(hidden, out_grad, basis_in, basis_out, eigen):
    own_tok, width = hidden.shape
    tokens = out_grad.shape[0]
    inner, depth = basis_in.shape
    rows, cols = basis_out.shape
    wide = width // NZ_LO
    chunk = wide // NY
    half = tokens // NC
    tall, broad = half // 2, depth // 4
    share = tokens // NX
    any_spec = pl.BlockSpec(memory_space=pl.ANY)
    vmem = pltpu.VMEM
    sems = 256
    return pl.pallas_call(
        kernel,
        out_shape=jax.ShapeDtypeStruct((rows, width), F32),
        in_specs=[any_spec] * 5,
        out_specs=pl.BlockSpec(memory_space=pltpu.VMEM),
        scratch_shapes=[
            vmem(hidden.shape, BF16),
            vmem(out_grad.shape, BF16),
            vmem(eigen.shape, F32),
            vmem((NC, inner, depth), BF16),
            vmem((NZ_LO, own_tok, wide), BF16),
            vmem((NZ_LO, own_tok, wide), BF16),
            vmem((NZ, tall, broad), BF16),
            vmem((NZ, tall, broad), BF16),
            vmem((NX, tall, broad), BF16),
            vmem((NZ, tall, broad), BF16),
            vmem((NC, half, depth), BF16),
            vmem((NX, share, cols), BF16),
            vmem((NX, share, cols), BF16),
            vmem((NY, share, cols), BF16),
            vmem((NZ, share, cols), BF16),
            vmem((NX, share, NZ_LO * cols), BF16),
            vmem((NX, NZ, rows, cols), BF16),
            vmem((NX, NZ, rows, cols), BF16),
            vmem((depth, NZ_LO * cols), BF16),
            vmem((NY, chunk, NZ_LO * cols), BF16),
            vmem((NY // 2, chunk, NZ_LO * cols), BF16),
            vmem((NY // 2 - 1, chunk, NZ_LO * cols), BF16),
            vmem((NY, chunk, NZ_LO * cols), BF16),
            vmem((NX * NZ_HI * rows, NZ_LO * cols), BF16),
            vmem((NZ_LO * NC, rows, wide), F32),
            vmem((NZ_LO, rows, wide), BF16),
            vmem((NZ_LO, rows, wide), BF16),
            vmem((NZ_LO, rows, wide), BF16),
            vmem((NZ_LO, rows, wide), BF16),
            pltpu.SemaphoreType.DMA((5,)),
            pltpu.SemaphoreType.DMA((sems,)),
            pltpu.SemaphoreType.DMA((sems,)),
        ],
        compiler_params=pltpu.CompilerParams(collective_id=0, has_side_effects=True),
    )(hidden, out_grad, basis_in, basis_out, eigen)


def solution(mesh):
    placed = (
        P("col", "row"),
        P(None, ("tp", "row")),
        P(("row", "col"), "tp"),
        P(("tp", "row"), "col"),
        P(("tp", "row"), "col"),
    )
    return jax.shard_map(
        shards, mesh=mesh, in_specs=placed, out_specs=P(("tp", "col"), "row"), check_vma=False
    )
```

time: 335 us -> 77.9 us (0.23)
  blocking collectives: 166 us -> 0 us
  waiting for transfers between devices: 132 us -> 0 us
  Pallas kernels: 0 us -> 74.4 us
  between operations: 13.5 us -> 0.01 us
  starting transfers between devices: 8.52 us -> 0 us
  matrix products: 4.45 us -> 0 us
    all_to_all x6 -> x0, blocking collectives: 166 us -> none  [the longest x3 86.2 us: sent_and_summed(): lax.all_to_all(tiles, axis, split_axis=0, concat_axis=0, tiled=True)]
    all_gather x1 -> x0, waiting for transfers between devices: 104 us -> none  [shards(): grad_full = lax.all_gather(out_grad, ('tp', 'row'), axis=1, tiled=True)]
    pallas_call x0 -> x1, Pallas kernels: none -> 74.4 us  [shards(): pl.pallas_call(kernel, out_shape=jax.ShapeDtypeStruct((rows, width), F32)...]
    all_to_all x1 -> x0, waiting for transfers between devices: 27.8 us -> none  [sent_to_all(): lax.all_to_all(jnp.broadcast_to(array[None], (devices, *array.shape)), ax...]
    all_to_all x1 -> x0, starting transfers between devices: 8.48 us -> none  [sent_to_all(): lax.all_to_all(jnp.broadcast_to(array[None], (devices, *array.shape)), ax...]
    dot_general x4 -> x0, matrix products: 4.45 us -> none  [the longest x1 1.82 us: contract_rows(): lax.dot_general(left, right, (((0,), (0,)), ((), ())), preferred_element_...]
  transfers between devices with their start and end apart: 2 -> 0, of which waited for: 2 -> 0; matrix products, arithmetic and copies ran while one was open for 0% -> 0% of each run, Pallas kernels for 0% -> 0%
where the time goes in v1:
time: 77.9 us; the launch traced here: 77.6 us
  Pallas kernels  74.4 us (96%)
  local copies, waits for them, and re-layouts  3.25 us (4%)
    pallas_call x1, Pallas kernels, shards(): pl.pallas_call(kernel, out_shape=jax.ShapeDtypeStruct((rows, width), F32)...  74.4 us
    unnamed x2, local copies, waits for them, and re-layouts  3.25 us

profile of v1, /device:TPU:1, one launch (start us, length us, event | category | flops | bytes accessed | tf_op | source)
XLA Modules:
  0.0 77.6 jit_solution(13802215482172485441)
XLA Ops:
  0.0 1.4 %copy.6.out_grad = bf16[128,64]{1,0:T(8,128)(2,1)} copy(bf16[128,64]{0,1:T(8,128)(2,1)} %param.6) | data formatting | bytes 32768 | tf_op args[1]
  1.4 74.4 %shard_map.55 = f32[64,1792]{1,0:T(8,128)} custom-call(bf16[16,1792]{1,0:T(8,128)(2,1)} %hidden.1, bf16[128,64]{1,0:T(8,128)(2,1)} %copy.6.out_grad, bf16[224,512]{1,0:T(8,128)(2,1)} %basis_in.1, bf16[64,128]{1,0:T(8,128)(2,1)} %basis_out.1, f32[64,128]{1,0:T(8,128)} %eigen.1), custom_call_target="tpu_custom_call" | custom-call | tf_op jit(solution)/shard_map/pallas_call | solution.py:353
  75.8 1.8 %copy.8 = f32[64,1792]{1,0:T(8,128)} copy(f32[64,1792]{1,0:T(8,128)} %shard_map.55) | data formatting | bytes 917504

commit v2 on v1

v2 whole, which is shorter than its diff:
```python
import functools

import jax
import jax.numpy as jnp
from jax import lax
from jax.experimental import pallas as pl
from jax.experimental.pallas import tpu as pltpu
from jax.sharding import PartitionSpec as P

MESH = pl.DeviceIdType.MESH
BF16 = jnp.bfloat16
F32 = jnp.float32
damping = 0.01
NX, NZ_HI, NZ_LO, NC = 4, 2, 4, 2
NZ = NZ_HI * NZ_LO
NY = 8
PIECES = ((0, 64), (64, 64), (128, 48), (176, 48))
BLOCKS = ((0, 128), (128, 96))


def far_first(count):
    return sorted(range(1, count), key=lambda hop: -min(hop, count - hop))


def kernel(
    hidden, out_grad, basis_in, basis_out, eigen, out,
    hid_v, grad_v, eig_v, basis, hid_s, hid_r,
    p_s, p_r, p_x, p_g, rin,
    r_s, r_r, r_y, r_z, r_x,
    e_g, b_g, rin_t, scaled, w_s, w_1, w_2, w_g, b_full, f_s, f_r,
    load_sem, send_sem, recv_sem,
):
    t = lax.axis_index("tp")
    row = lax.axis_index("row")
    col = lax.axis_index("col")
    z_hi, x = lax.div(row, NX), lax.rem(row, NX)
    z_lo, core = lax.div(col, NC), lax.rem(col, NC)
    z = z_hi * NZ_LO + z_lo

    def at_y(pos):
        return {"tp": pos}

    def at_x(pos):
        return {"row": z_hi * NX + pos}

    def at_z(pos):
        return {
            "row": lax.div(pos, NZ_LO) * NX + x,
            "col": lax.rem(pos, NZ_LO) * NC + core,
        }

    def at_zlo(pos):
        return {"col": pos * NC + core}

    def at_col(pos):
        return {"col": pos}

    at_core = {"col": z_lo * NC + 1 - core}

    slots = [0, 0]
    sent = []

    def fresh(kind, count):
        first = slots[kind]
        slots[kind] += count
        return first

    def remote(src, dst, send, recv, device):
        return pltpu.make_async_remote_copy(
            src_ref=src, dst_ref=dst, send_sem=send_sem.at[send], recv_sem=recv_sem.at[recv],
            device_id=device, device_id_type=MESH,
        )

    def exchange(src, dst, every, me, count, at):
        send, recv = fresh(0, 1), fresh(1, 1)
        for hop in far_first(count):
            peer = lax.rem(me + hop, count)
            remote(src(peer), dst(me), send, recv, at(peer)).start()
        whole = remote(every, every, send, recv, at(lax.rem(me + 1, count)))
        sent.append(whole)
        return whole.wait_recv

    def gather(buf, me, count, at):
        part = buf.at[me]
        return exchange(
            lambda peer: part, lambda mine: part, buf.at[pl.ds(0, count - 1)], me, count, at
        )

    def scatter(src, dst, me, count, at):
        return exchange(
            lambda peer: src.at[peer], lambda mine: dst.at[mine], dst.at[pl.ds(0, count - 1)],
            me, count, at,
        )

    def to_core(ref, other):
        send, recv = fresh(0, 1), fresh(1, 1)
        copy = remote(ref, ref, send, recv, at_core)
        copy.start()
        sent.append(copy)
        return remote(other, other, send, recv, at_core).wait_recv

    def total(buf, count):
        acc = buf[0].astype(F32)
        for i in range(1, count):
            acc = acc + buf[i].astype(F32)
        return acc

    def put(buf, pos, value):
        buf[pl.ds(pos, 1)] = value[None]

    e_own, b_own = e_g.at[core], b_g.at[core]
    loads = [
        pltpu.make_async_copy(hidden, hid_v, load_sem.at[0]),
        pltpu.make_async_copy(out_grad, grad_v, load_sem.at[1]),
        pltpu.make_async_copy(basis_out, b_own.at[x, z], load_sem.at[2]),
        pltpu.make_async_copy(basis_in, basis.at[core], load_sem.at[3]),
        pltpu.make_async_copy(eigen, eig_v, load_sem.at[4]),
    ]
    for load in loads:
        load.start()

    barrier = pltpu.get_barrier_semaphore()
    partners = [at_core]
    partners += [at_x(lax.rem(x + hop, NX)) for hop in range(1, NX)]
    partners += [at_z(lax.rem(z + hop, NZ)) for hop in range(1, NZ)]
    partners += [at_y(lax.rem(t + hop, NY)) for hop in range(1, NY)]
    partners += [
        at_col(lax.rem(z_lo + hop, NZ_LO) * NC + 1 - core) for hop in range(1, NZ_LO)
    ]
    for partner in partners:
        pl.semaphore_signal(barrier, inc=1, device_id=partner, device_id_type=MESH)

    own_tok = hid_v.shape[0]
    wide = hid_s.shape[2]
    loads[0].wait()
    hid = hid_v[...]
    for i in range(NZ_LO):
        hid_s[i] = hid[:, i * wide:(i + 1) * wide]
    hid_r[pl.ds(z_lo, 1)] = hid_s[pl.ds(z_lo, 1)]

    loads[1].wait()
    loads[2].wait()
    part = lax.dot_general(
        grad_v[...], b_g[core, x, z], (((0,), (0,)), ((), ())), preferred_element_type=F32
    )
    order = [i * NC + p for p in range(NC) for i in range(NZ_LO)]
    part = jnp.concatenate([part[i * own_tok:(i + 1) * own_tok] for i in order], axis=0)
    piece = r_s.shape[1]
    for i in range(NX):
        r_s[i] = part[i * piece:(i + 1) * piece].astype(BF16)
    r_r[pl.ds(x, 1)] = r_s[pl.ds(x, 1)]
    loads[3].wait()
    loads[4].wait()
    queries = own_tok * NZ_LO * NC
    e_g[core, x, z] = (1.0 / (queries * (eig_v[...] + damping))).astype(BF16)

    pl.semaphore_wait(barrier, len(partners))

    hid_done = scatter(hid_s, hid_r, z_lo, NZ_LO, at_zlo)
    basis_done = to_core(basis.at[core], basis.at[1 - core])
    r_done = scatter(r_s, r_r, x, NX, at_x)

    def zgather(buf):
        part = buf.at[x, z]
        return exchange(
            lambda peer: part, lambda mine: part, buf.at[x, pl.ds(0, NZ - 1)], z, NZ, at_z
        )

    ez_done = zgather(e_own)

    r_done()
    put(r_y, t, total(r_r, NX).astype(BF16))
    ry_done = gather(r_y, t, NY, at_y)

    hid_done()
    basis_done()
    deep = NC * basis.shape[1]
    depth = basis.shape[2]
    p_full = jnp.dot(
        hid_r[...].reshape(NZ_LO * own_tok, wide), basis[...].reshape(deep, depth),
        preferred_element_type=F32,
    )
    tall, broad = p_s.shape[1:]
    across = depth // broad
    for i in range(NZ):
        h, q = i // across, i % across
        p_s[i] = p_full[h * tall:(h + 1) * tall, q * broad:(q + 1) * broad].astype(BF16)
    p_r[pl.ds(z, 1)] = p_s[pl.ds(z, 1)]
    p_done = scatter(p_s, p_r, z, NZ, at_z)

    ry_done()
    put(r_z, z, total(r_y, NY).astype(BF16))
    rz_done = gather(r_z, z, NZ, at_z)

    p_done()
    put(p_x, x, total(p_r, NZ).astype(BF16))
    px_done = gather(p_x, x, NX, at_x)

    ez_done()
    ex_done = gather(e_own, x, NX, at_x)

    px_done()
    put(p_g, z, total(p_x, NX).astype(BF16))
    pg_done = gather(p_g, z, NZ, at_z)

    rz_done()
    put(
        r_x.at[core], x,
        jnp.concatenate(
            [
                sum(r_z[h * NZ_LO + i].astype(F32) for h in range(NZ_HI)).astype(BF16)
                for i in range(NZ_LO)
            ],
            axis=1,
        ),
    )
    rx_done = gather(r_x.at[core], x, NX, at_x)

    pg_done()
    put(
        rin, core,
        jnp.concatenate(
            [
                jnp.concatenate([p_g[h * across + q] for q in range(across)], axis=1)
                for h in range(NZ // across)
            ],
            axis=0,
        ),
    )
    rin_done = to_core(rin.at[core], rin.at[1 - core])
    rx_done()
    ro_done = to_core(r_x.at[core], r_x.at[1 - core])
    ex_done()
    e_done = to_core(e_own, e_g.at[1 - core])
    bz_done = zgather(b_own)

    rin_done()
    rin_t[...] = rin[...].reshape(queries, depth).T
    ro_done()
    e_done()

    rows, cols = b_g.shape[3:]
    inner = basis.shape[1]
    heading = 1 - 2 * core
    ahead = at_y(lax.rem(t + heading + NY, NY))
    behind = at_y(lax.rem(t - heading + NY, NY))
    first_hops, second_hops = NY // 2, NY // 2 - 1

    def off(steps):
        return lax.rem(t + heading * steps + 2 * NY, NY)

    own_basis = basis[core]

    def form(dest):
        low, par = lax.div(dest, NC), lax.rem(dest, NC)
        lanes = pl.ds(pl.multiple_of(low * cols, cols), cols)
        coeff = jnp.dot(
            rin_t[...], r_x[par, :, :, lanes].reshape(queries, cols), preferred_element_type=F32
        )
        for h in range(NZ_HI):
            for i in range(NX):
                r0 = (h * NX + i) * rows
                scaled[r0:r0 + rows] = (
                    coeff[r0:r0 + rows] * e_g[par, i, h * NZ_LO + low].astype(F32)
                ).astype(BF16)
        put(
            w_s, dest,
            jnp.dot(own_basis, scaled[...], preferred_element_type=F32).astype(BF16),
        )

    count = len(PIECES)

    def cut(buf, slot, q):
        return buf.at[slot, pl.ds(*PIECES[q])]

    def add_in(slot, buf, step, q):
        here = (pl.ds(slot, 1), pl.ds(*PIECES[q]))
        there = (pl.ds(step, 1), pl.ds(*PIECES[q]))
        w_s[here] = (w_s[here].astype(F32) + buf[there].astype(F32)).astype(BF16)

    ring = fresh(0, 1)
    sem_1 = fresh(1, first_hops * count)
    sem_2 = fresh(1, second_hops * count)

    def arrive_1(step, q):
        slot = cut(w_1, step, q)
        remote(slot, slot, ring, sem_1 + step * count + q, behind).wait_recv()

    def arrive_2(step, q):
        slot = cut(w_2, step, q)
        remote(slot, slot, ring, sem_2 + step * count + q, ahead).wait_recv()

    def leave_1(dest, step, q):
        remote(
            cut(w_s, dest, q), cut(w_1, step, q), ring, sem_1 + step * count + q, ahead
        ).start()

    def leave_2(dest, step, q):
        remote(
            cut(w_s, dest, q), cut(w_2, step, q), ring, sem_2 + step * count + q, behind
        ).start()

    form(off(first_hops))
    for q in range(count):
        leave_1(off(first_hops), 0, q)
    form(off(-second_hops))
    for q in range(count):
        leave_2(off(-second_hops), 0, q)
    for step in range(first_hops - 1, 0, -1):
        form(off(step))
        if step > 1:
            form(off(1 - step))
    form(t)
    for step in range(1, first_hops):
        for q in range(count):
            dest = off(first_hops - step)
            arrive_1(step - 1, q)
            add_in(dest, w_1, step - 1, q)
            leave_1(dest, step, q)
            if step < second_hops:
                dest = off(step - second_hops)
                arrive_2(step - 1, q)
                add_in(dest, w_2, step - 1, q)
                leave_2(dest, step, q)
    sent.append(
        remote(
            w_s.at[pl.ds(0, NY - 1)], w_s.at[pl.ds(0, NY - 1)], ring, sem_1, ahead
        )
    )
    bz_done()
    bx_done = gather(b_own, x, NX, at_x)

    round_ = fresh(0, 1)
    gsem_1 = fresh(1, first_hops * count)
    gsem_2 = fresh(1, second_hops * count)

    def pass_on(slot, sem, q, device):
        return remote(cut(w_g, slot, q), cut(w_g, slot, q), round_, sem + q, device)

    for q in range(count):
        arrive_2(second_hops - 1, q)
        add_in(t, w_2, second_hops - 1, q)
        arrive_1(first_hops - 1, q)
        here = (pl.ds(t, 1), pl.ds(*PIECES[q]))
        there = (pl.ds(first_hops - 1, 1), pl.ds(*PIECES[q]))
        w_g[here] = (w_s[here].astype(F32) + w_1[there].astype(F32)).astype(BF16)
        pass_on(t, gsem_1, q, ahead).start()
        pass_on(t, gsem_2, q, behind).start()
    bx_done()
    b_done = to_core(b_own, b_g.at[1 - core])
    for step in range(1, first_hops + 1):
        if step == first_hops:
            b_done()
            for p in range(NC):
                for i in range(NX):
                    for k in range(NZ):
                        h, low = k // NZ_LO, k % NZ_LO
                        r0, c0 = (h * NX + i) * rows, (low * NC + p) * cols
                        b_full[r0:r0 + rows, c0:c0 + cols] = b_g[p, i, k]
        for q in range(count):
            slot = off(-step)
            pass_on(slot, gsem_1 + (step - 1) * count, q, behind).wait_recv()
            if step < first_hops:
                pass_on(slot, gsem_1 + step * count, q, ahead).start()
            if step <= second_hops:
                slot = off(step)
                pass_on(slot, gsem_2 + (step - 1) * count, q, ahead).wait_recv()
                if step < second_hops:
                    pass_on(slot, gsem_2 + step * count, q, behind).start()
    sent.append(
        remote(
            w_g.at[pl.ds(0, NY - 1)], w_g.at[pl.ds(0, NY - 1)], round_, gsem_1, ahead
        )
    )

    f_done = []
    for n, (f0, size) in enumerate(BLOCKS):
        w_all = jnp.concatenate([w_g[i, f0:f0 + size] for i in range(NY)], axis=1)
        result = lax.dot_general(
            b_full[...], w_all, (((1,), (1,)), ((), ())), preferred_element_type=F32
        ).astype(BF16)
        for i in range(NZ_LO * NC):
            f_s[n, i, :, :size] = result[i * rows:(i + 1) * rows]
        f_r[n, pl.ds(col, 1)] = f_s[n, pl.ds(col, 1)]
        f_done.append(scatter(f_s.at[n], f_r.at[n], col, NZ_LO * NC, at_col))
    for n, (f0, size) in enumerate(BLOCKS):
        f_done[n]()
        for i in range(NZ_LO * NC):
            out[:, i * inner + f0:i * inner + f0 + size] = f_r[n, i, :, :size].astype(F32)
    for copy in sent:
        copy.wait_send()


def shards(hidden, out_grad, basis_in, basis_out, eigen):
    out_grad = out_grad.T
    own_tok, width = hidden.shape
    tokens = out_grad.shape[1]
    inner, depth = basis_in.shape
    rows, cols = basis_out.shape
    wide = width // NZ_LO
    half = tokens // NC
    tall, broad = half // 2, depth // 4
    share = tokens // NX
    every = NC * NZ_LO * cols
    any_spec = pl.BlockSpec(memory_space=pl.ANY)
    vmem = pltpu.VMEM
    return pl.pallas_call(
        kernel,
        out_shape=jax.ShapeDtypeStruct((rows, width), F32),
        in_specs=[any_spec] * 5,
        out_specs=pl.BlockSpec(memory_space=pltpu.VMEM),
        scratch_shapes=[
            vmem(hidden.shape, BF16),
            vmem(out_grad.shape, BF16),
            vmem(eigen.shape, F32),
            vmem((NC, inner, depth), BF16),
            vmem((NZ_LO, own_tok, wide), BF16),
            vmem((NZ_LO, own_tok, wide), BF16),
            vmem((NZ, tall, broad), BF16),
            vmem((NZ, tall, broad), BF16),
            vmem((NX, tall, broad), BF16),
            vmem((NZ, tall, broad), BF16),
            vmem((NC, half, depth), BF16),
            vmem((NX, share, cols), BF16),
            vmem((NX, share, cols), BF16),
            vmem((NY, share, cols), BF16),
            vmem((NZ, share, cols), BF16),
            vmem((NC, NX, share, NZ_LO * cols), BF16),
            vmem((NC, NX, NZ, rows, cols), BF16),
            vmem((NC, NX, NZ, rows, cols), BF16),
            vmem((depth, tokens), BF16),
            vmem((depth, cols), BF16),
            vmem((NY, inner, cols), BF16),
            vmem((NY // 2, inner, cols), BF16),
            vmem((NY // 2 - 1, inner, cols), BF16),
            vmem((NY, inner, cols), BF16),
            vmem((NX * NZ_HI * rows, every), BF16),
            vmem((len(BLOCKS), NZ_LO * NC, rows, BLOCKS[0][1]), BF16),
            vmem((len(BLOCKS), NZ_LO * NC, rows, BLOCKS[0][1]), BF16),
            pltpu.SemaphoreType.DMA((5,)),
            pltpu.SemaphoreType.DMA((24,)),
            pltpu.SemaphoreType.DMA((24 + 2 * (NY - 1) * len(PIECES),)),
        ],
        compiler_params=pltpu.CompilerParams(collective_id=0, has_side_effects=True),
    )(hidden, out_grad, basis_in, basis_out, eigen)


def solution(mesh):
    placed = (
        P("col", "row"),
        P(None, ("tp", "row")),
        P(("row", "col"), "tp"),
        P(("tp", "row"), "col"),
        P(("tp", "row"), "col"),
    )
    return jax.shard_map(
        shards, mesh=mesh, in_specs=placed, out_specs=P(("tp", "col"), "row"), check_vma=False
    )
```

time: 77.9 us -> 72.7 us (0.933)
  Pallas kernels: 74.4 us -> 70.7 us
  local copies, waits for them, and re-layouts: 3.25 us -> 1.82 us
    pallas_call x1, Pallas kernels: 74.4 us -> 70.7 us  [shards(): pl.pallas_call(kernel, out_shape=jax.ShapeDtypeStruct((rows, width), F32)...]
    unnamed x2 -> x1, local copies, waits for them, and re-layouts: 3.25 us -> 1.82 us
where the time goes in v2:
time: 72.7 us; the launch traced here: 72.6 us
  Pallas kernels  70.7 us (97%)
  local copies, waits for them, and re-layouts  1.82 us (3%)
    pallas_call x1, Pallas kernels, shards(): pl.pallas_call(kernel, out_shape=jax.ShapeDtypeStruct((rows, width), F32)...  70.7 us
    unnamed x1, local copies, waits for them, and re-layouts  1.82 us

profile of v2, /device:TPU:1, one launch (start us, length us, event | category | flops | bytes accessed | tf_op | source)
XLA Modules:
  0.0 72.6 jit_solution(1877287836576209241)
XLA Ops:
  0.0 70.7 %shard_map.55 = f32[64,1792]{1,0:T(8,128)} custom-call(bf16[16,1792]{1,0:T(8,128)(2,1)} %hidden.1, bf16[64,128]{1,0:T(8,128)(2,1)} %bitcast.1, bf16[224,512]{1,0:T(8,128)(2,1)} %basis_in.1, bf16[64,128]{1,0:T(8,128)(2,1)} %basis_out.1, f32[64,128]{1,0:T(8,128)} %eigen.1), custom_call_target="tpu_custom_call" | custom-call | tf_op jit(solution)/shard_map/pallas_call | solution.py:407
  70.8 1.8 %copy.7 = f32[64,1792]{1,0:T(8,128)} copy(f32[64,1792]{1,0:T(8,128)} %shard_map.55) | data formatting | bytes 917504
